TPU v7x, 128 devices: a whole 4x4x4 slice. The times are simulated.
128 devices in a mesh: tok: 32 (over y_lo, z, x), voc: 4 (over y_hi, core).
Axes of the slice: x: 4, y: 4 (y_hi: 2, y_lo: 2; y = y_hi * 2 + y_lo), z: 4, core: 2. Of those that a mesh axis runs over, the one named last changes fastest.
Arguments:
- hidden: bfloat16 [1024, 3584], P('tok'), may hold values from -700 to 700
- teacher_logits: bfloat16 [1024, 81920], P(None, ('tok', 'voc')), may hold values from -300 to 300
- sampled_ids: int32 [1024], P('tok'), may hold values from 0 to 81919
- loss_mask: int32 [1024], P('tok'), may hold values from 0 to 1, as said below
- student_head: bfloat16 [3584, 81920], P(None, ('tok', 'voc')), may hold values from -0.3125 to 0.3125
Outputs:
- loss: float32 [], replicated
- sampled_ratio: float32 [1024], P(('tok', 'voc'))
- hidden_grad: bfloat16 [1024, 3584], P(('tok', 'voc'))
- head_grad: bfloat16 [3584, 81920], P(None, ('tok', 'voc'))
Inputs may be any that keep to these rules, and one draw needn't show every extreme that they name: `loss_mask`: at least one position is valid.
All inputs are finite; a program needn't handle non-finite values.
Results may differ from a plain program's by a relative error of at most 0.02.
Values may be sent and summed in bfloat16 or wider, within the bound.
No kernel may reach another device: no remote copies, remote signals or barrier semaphores. Data moves between devices by JAX's collectives and lax.ppermute only.
A program may use at most 128 MiB of HBM per device.

v0:
```python
import jax
import jax.numpy as jnp
from jax import lax
from jax.sharding import Mesh
from jax.sharding import PartitionSpec as P

TOK = ("tok_0", "tok_1", "tok_2")
TOK_VOC = ("tok_0", "tok_1", "tok_2", "voc_0", "voc_1")
VOC = ("voc_0", "voc_1")


def all_in_one(shard, axis):
    leaves = jax.tree.leaves(shard)
    order = sorted(range(len(leaves)), key=lambda k: -leaves[k].size)
    width = (1, *leaves[order[0]].shape)[-1]
    lines = [
        jnp.pad(leaves[k].reshape(-1), (0, -leaves[k].size % width)).reshape(-1, width)
        for k in order
    ]
    both, at, found = (lax.all_gather(jnp.concatenate(lines), axis), 0, {})
    for k, line in zip(order, lines):
        share = both[:, at : at + len(line)].reshape(len(both), -1)
        found[k] = share[:, : leaves[k].size].reshape(-1, *leaves[k].shape)
        at += len(line)
    numbers = iter(range(len(leaves)))
    return jax.tree.map(lambda _: found[next(numbers)], shard)


def combined_by_axis(shard, axes, combine):
    for axis in axes:
        pieces = all_in_one(shard, axis)
        shard = jax.tree.map(lambda part: part[0], pieces)
        for k in range(1, lax.axis_size(axis)):
            shard = combine(shard, jax.tree.map(lambda part: part[k], pieces))
    return shard


def sum_in_order(blocks, axes, order):
    inside = blocks.shape[1:]
    blocks = blocks.reshape(*(lax.axis_size(a) for a in axes), *inside)
    blocks = jnp.moveaxis(blocks, order, range(len(axes))).reshape(-1, *inside)
    for k in order:
        blocks = lax.psum_scatter(blocks, axes[k], scatter_dimension=0, tiled=True)
    return blocks[0]


def in_blocks(shard, dim, devices):
    before, after = (shard.shape[:dim], shard.shape[dim + 1 :])
    return jnp.moveaxis(shard.reshape(*before, devices, -1, *after), dim, 0)


def scatter_axes(shard, axes, order, dim):
    devices = lax.axis_size(axes)
    return sum_in_order(in_blocks(shard, dim, devices), axes, order)


def summed_on_arrival(shard, axis, dim):
    devices = lax.axis_size(axis)
    blocks = lax.all_to_all(in_blocks(shard, dim, devices), axis, 0, 0, tiled=True)
    return jnp.sum(blocks.astype(jnp.float32), axis=0)


def combine_stats(first, second):
    smax_a, stot_a, cross_a, tmax_a, ttot_a, spick_a, tpick_a = first
    smax_b, stot_b, cross_b, tmax_b, ttot_b, spick_b, tpick_b = second
    student_max = jnp.maximum(smax_a, smax_b)
    teacher_max = jnp.maximum(tmax_a, tmax_b)
    factor_a = jnp.exp(smax_a - student_max)
    factor_b = jnp.exp(smax_b - student_max)
    student_total = stot_a * factor_a + stot_b * factor_b
    cross_term = cross_a * factor_a + cross_b * factor_b
    teacher_total = ttot_a * jnp.exp(tmax_a - teacher_max) + ttot_b * jnp.exp(tmax_b - teacher_max)
    return (
        student_max,
        student_total,
        cross_term,
        teacher_max,
        teacher_total,
        spick_a + spick_b,
        tpick_a + tpick_b,
    )


def per_device(hidden, teacher_logits, sampled_ids, loss_mask, student_head):
    all_hidden, all_ids, all_mask = (
        lax.all_gather(hidden, TOK, axis=0, tiled=True),
        lax.all_gather(sampled_ids, TOK, axis=0, tiled=True),
        lax.all_gather(loss_mask, TOK, axis=0, tiled=True),
    )
    teacher = teacher_logits.astype(jnp.float32)
    student = jnp.dot(all_hidden, student_head, preferred_element_type=jnp.float32)
    devices = lax.axis_size(TOK_VOC)
    position = lax.axis_index(TOK_VOC)
    vocab_dev = student_head.shape[1]
    rows_all = all_hidden.shape[0]
    rows_own = rows_all // devices
    weight = all_mask.astype(jnp.float32)
    count = jnp.sum(weight)
    columns = position * vocab_dev + lax.broadcasted_iota(jnp.int32, (1, vocab_dev), 1)
    chosen = all_ids[:, None] == columns
    local_smax = jnp.max(student, axis=1)
    local_tmax = jnp.max(teacher, axis=1)
    shifted = jnp.exp(student - local_smax[:, None])
    local_stats = (
        local_smax,
        jnp.sum(shifted, axis=1),
        jnp.sum(shifted * (student - teacher), axis=1),
        local_tmax,
        jnp.sum(jnp.exp(teacher - local_tmax[:, None]), axis=1),
        jnp.sum(jnp.where(chosen, student, 0.0), axis=1),
        jnp.sum(jnp.where(chosen, teacher, 0.0), axis=1),
    )
    merged = combined_by_axis(local_stats, TOK_VOC, combine_stats)
    (
        student_max,
        student_total,
        cross_term,
        teacher_max,
        teacher_total,
        student_pick,
        teacher_pick,
    ) = merged
    student_shift = student_max + jnp.log(student_total)
    teacher_shift = teacher_max + jnp.log(teacher_total)
    row_kl = cross_term / student_total - student_shift + teacher_shift
    ratio_all = student_pick - student_shift - (teacher_pick - teacher_shift)
    sampled_ratio = lax.dynamic_slice_in_dim(ratio_all, position * rows_own, rows_own, 0)
    student_log = student - student_shift[:, None]
    differ = student_log - (teacher - teacher_shift[:, None])
    dlogits = (weight[:, None] * jnp.exp(student_log) * (differ - row_kl[:, None])).astype(
        jnp.bfloat16
    )
    loss = jnp.sum(weight * row_kl) / count
    partial_sum = scatter_axes(
        lax.dot_general(
            dlogits, student_head, (((1,), (1,)), ((), ())), preferred_element_type=jnp.float32
        ).astype(jnp.bfloat16),
        TOK,
        (1, 2, 0),
        0,
    ).astype(jnp.float32)
    hidden_sum = summed_on_arrival(partial_sum.astype(jnp.bfloat16), VOC, 0)
    hidden_grad = hidden_sum.astype(jnp.bfloat16)
    head_grad = lax.dot_general(
        all_hidden, dlogits, (((0,), (0,)), ((), ())), preferred_element_type=jnp.float32
    ).astype(jnp.bfloat16)
    return (loss, sampled_ratio, hidden_grad, head_grad)


def solution(mesh):
    split = Mesh(mesh.devices.reshape(2, 4, 4, 2, 2), ("tok_0", "tok_1", "tok_2", "voc_0", "voc_1"))
    in_specs = (P(TOK, None), P(None, TOK_VOC), P(TOK), P(TOK), P(None, TOK_VOC))
    out_specs = (P(), P(TOK_VOC), P(TOK_VOC, None), P(None, TOK_VOC))
    return jax.shard_map(
        per_device, mesh=split, in_specs=in_specs, out_specs=out_specs, check_vma=False
    )
```

profile of v0, /device:TPU:1, one launch (start us, length us, event | category | flops | bytes accessed | tf_op | source)
XLA Modules:
  0.0 395.3 jit_solution(10163011717840257338)
XLA Ops:
  7.2 0.0 copy-start.4
  7.2 0.0 copy-start.1
  7.2 0.0 copy-start.2
  7.2 0.0 copy-start.3
  7.2 0.0 all-gather.12.cloned.1.call-start
  7.3 0.7 all-gather.12.cloned.1.call-update
  7.9 0.0 reduce-scatter.4.cloned.1.call-start
  8.0 1.6 copy.14
  9.6 0.0 copy-done.1
  9.6 0.2 reduce_max.28
  9.9 0.0 copy-done.4
  9.9 0.6 dynamic-slice
  11.1 0.0 copy-done.2
  11.2 0.2 dynamic-update-slice
  11.4 0.0 copy-done.3
  11.4 0.2 dynamic-update-slice.1
  11.6 17.6 %all-reduce.2 = (s32[1024]{0:T(1024)S(1)}, s32[1024]{0:T(1024)S(1)}) all-reduce(s32[1024]{0:T(1024)S(1)} %dynamic-update-slice, s32[1024]{0:T(1024)S(1)} %dynamic-update-slice.1), channel_id=1, replica_groups=mesh['tok_0'=2,'tok_1'=4,'tok_2'=4,'voc_0'=2,'voc_1'=2] {'tok_0','tok_1'..., use_global_device_ids=true, to_apply=%add | all-reduce | flops 2048 | bytes 16384
  29.3 127.6 %all-gather.12.cloned.1.call-done = bf16[1024,3584]{1,0:T(8,128)(2,1)} async-done(((bf16[32,3584]{1,0:T(8,128)(2,1)}), bf16[1024,3584]{1,0:T(8,128)(2,1)}) %all-gather.12.cloned.1.call-update) | async-done | bytes 7340048 | tf_op jit(solution)/shard_map/all_gather | solution.py:86
  156.9 8.6 %fusion.119 = (f32[1024]{0:T(1024)S(1)}, f32[1024,640]{0,1:T(8,128)S(1)}) fusion(bf16[1024,3584]{1,0:T(8,128)(2,1)} %all-gather.12.cloned.1.call-done, bf16[3584,640]{1,0:T(8,128)(2,1)} %param.9), kind=kOutput, calls=%fused_computation.224 | convolution fusion | flops 4698274816 | bytes 14553088 | tf_op jit(solution)/shard_map/dot_general | solution.py:91
  165.5 0.0 copy-start
  165.6 1.5 copy-done
  167.0 1.8 fusion.3
  168.8 0.1 concatenate.15
  168.9 3.8 all-gather.5
  172.8 0.1 concatenate.16
  172.9 9.1 %all-gather.6 = f32[4,7,1024]{2,1,0:T(8,128)S(1)} all-gather(f32[1,7,1024]{2,1,0:T(8,128)S(1)} %bitcast.598), channel_id=3, replica_groups=mesh['tok_0'=2,'tok_1'=4,'tok_2'=4,'voc_0'=2,'voc_1'=2] {'tok_1'}, dimensions={0}, use_global_device_ids=true | all-gather | bytes 143360 | tf_op jit(solution)/shard_map/all_gather | solution.py:20
  182.0 0.1 fusion.55
  182.1 0.1 fusion.73
  182.2 0.1 concatenate.17
  182.2 9.1 %all-gather.7 = f32[4,7,1024]{2,1,0:T(8,128)S(1)} all-gather(f32[1,7,1024]{2,1,0:T(8,128)S(1)} %bitcast.599), channel_id=4, replica_groups=mesh['tok_0'=2,'tok_1'=4,'tok_2'=4,'voc_0'=2,'voc_1'=2] {'tok_2'}, dimensions={0}, use_global_device_ids=true | all-gather | bytes 143360 | tf_op jit(solution)/shard_map/all_gather | solution.py:20
  191.4 0.1 fusion.26
  191.5 0.1 fusion.44
  191.5 0.1 concatenate.18
  191.6 4.9 %all-gather.8 = f32[2,7,1024]{2,1,0:T(8,128)S(1)} all-gather(f32[1,7,1024]{2,1,0:T(8,128)S(1)} %bitcast.600), channel_id=5, replica_groups=mesh['tok_0'=2,'tok_1'=4,'tok_2'=4,'voc_0'=2,'voc_1'=2] {'voc_0'}, dimensions={0}, use_global_device_ids=true | all-gather | bytes 86016 | tf_op jit(solution)/shard_map/all_gather | solution.py:20
  196.6 0.1 concatenate.19
  196.7 30.3 %all-gather.9 = f32[2,7,1024]{2,1,0:T(8,128)S(1)} all-gather(f32[1,7,1024]{2,1,0:T(8,128)S(1)} %bitcast.601), channel_id=6, replica_groups=mesh['tok_0'=2,'tok_1'=4,'tok_2'=4,'voc_0'=2,'voc_1'=2] {'voc_1'}, dimensions={0}, use_global_device_ids=true | all-gather | bytes 86016 | tf_op jit(solution)/shard_map/all_gather | solution.py:20
  227.1 0.6 convert_reduce_fusion
  227.7 2.6 fusion.10
  230.2 8.5 %convolution_convert_fusion = bf16[1024,3584]{1,0:T(8,128)(2,1)S(1)} fusion(bf16[1024,640]{0,1:T(8,128)(2,1)S(1)} %fusion.10, bf16[3584,640]{1,0:T(8,128)(2,1)} %param.9), kind=kOutput, calls=%fused_computation | convolution fusion | flops 4701290496 | bytes 13238272 | tf_op jit(solution)/shard_map/dot_general | solution.py:135
  238.7 3.8 copy.15
  242.5 0.0 reduce-scatter.4.cloned.1.call-update
  242.6 0.0 reduce-scatter.6.cloned.1.call-start
  242.6 72.9 %reduce-scatter.4.cloned.1.call-done = bf16[8,32,3584]{2,1,0:T(8,128)(2,1)} async-done(((bf16[32,32,3584]{2,1,0:T(8,128)(2,1)}), bf16[8,32,3584]{2,1,0:T(8,128)(2,1)}) %reduce-scatter.4.cloned.1.call-update) | async-done | bytes 1835024 | tf_op jit(solution)/shard_map/reduce_scatter | solution.py:43
  315.5 0.0 reduce-scatter.6.cloned.1.call-update
  315.5 0.0 reduce-scatter.8.cloned.1.call-start
  315.6 29.5 %reduce-scatter.6.cloned.1.call-done = bf16[2,32,3584]{2,1,0:T(8,128)(2,1)} async-done(((bf16[8,32,3584]{2,1,0:T(8,128)(2,1)}), bf16[2,32,3584]{2,1,0:T(8,128)(2,1)}) %reduce-scatter.6.cloned.1.call-update) | async-done | bytes 458768 | tf_op jit(solution)/shard_map/reduce_scatter | solution.py:43
  345.1 0.0 reduce-scatter.8.cloned.1.call-update
  345.1 18.3 %reduce-scatter.8.cloned.1.call-done = bf16[1,32,3584]{2,1,0:T(8,128)(2,1)} async-done(((bf16[2,32,3584]{2,1,0:T(8,128)(2,1)}), bf16[1,32,3584]{2,1,0:T(8,128)(2,1)}) %reduce-scatter.8.cloned.1.call-update) | async-done | bytes 229392 | tf_op jit(solution)/shard_map/reduce_scatter | solution.py:43
  363.4 4.8 %all-to-all-start = ((bf16[4,8,3584]{2,1,0:T(8,128)(2,1)}), bf16[4,8,3584]{2,1,0:T(8,128)(2,1)S(1)}, u32[]{:S(2)}, u32[]{:S(2)}) async-start(bf16[4,8,3584]{2,1,0:T(8,128)(2,1)} %bitcast.596), calls=%async_computation.3 | async-start | bytes 458752 | tf_op jit(solution)/shard_map/all_to_all | solution.py:59
  368.2 9.6 %fusion = bf16[3584,640]{0,1:T(8,128)(2,1)} fusion(bf16[1024,640]{0,1:T(8,128)(2,1)S(1)} %fusion.10, bf16[1024,3584]{1,0:T(8,128)(2,1)} %all-gather.12.cloned.1.call-done), kind=kOutput, calls=%fused_computation.2 | convolution fusion | flops 4699914240 | bytes 13238272 | tf_op jit(solution)/shard_map/dot_general | solution.py:144
  377.8 7.2 %copy.16 = bf16[3584,640]{1,0:T(8,128)(2,1)} copy(bf16[3584,640]{0,1:T(8,128)(2,1)} %fusion) | data formatting | bytes 9175040
  386.4 0.6 dynamic_slice.3
  387.0 0.0 all-to-all-done
  387.0 0.7 reduce_sum.82
  (15 shorter events, 0.3 us)
Async XLA Ops:
  7.2 2.7 copy-start.4
  7.2 2.4 copy-start.1
  7.2 4.0 %copy-start.2 = (s32[32]{0:T(128)S(1)}, s32[32]{0:T(128)}, u32[]{:S(2)}) copy-start(s32[32]{0:T(128)} %param.8) | copy-start | bytes 388
  7.2 4.2 %copy-start.3 = (s32[32]{0:T(128)S(1)}, s32[32]{0:T(128)}, u32[]{:S(2)}) copy-start(s32[32]{0:T(128)} %param.7) | copy-start | bytes 388
  7.2 149.7 %all-gather.12.cloned.1.call-start = ((), (), s32[]{:S(2)}) async-start(), calls=%async_computation.4 | async-start | bytes 7569408 | tf_op jit(solution)/shard_map/all_gather | solution.py:86
  7.9 307.6 %reduce-scatter.4.cloned.1.call-start = ((), (), s32[]{:S(2)}) async-start(), calls=%async_computation.5 | async-start | bytes 9175040 | tf_op jit(solution)/shard_map/reduce_scatter | solution.py:43
  165.5 1.5 copy-start
  242.6 102.5 %reduce-scatter.6.cloned.1.call-start = ((), (), s32[]{:S(2)}) async-start(), calls=%async_computation.6 | async-start | bytes 2293760 | tf_op jit(solution)/shard_map/reduce_scatter | solution.py:43
  315.5 47.9 %reduce-scatter.8.cloned.1.call-start = ((), (), s32[]{:S(2)}) async-start(), calls=%async_computation.7 | async-start | bytes 688128 | tf_op jit(solution)/shard_map/reduce_scatter | solution.py:43
  363.4 23.6 %all-to-all-start = ((bf16[4,8,3584]{2,1,0:T(8,128)(2,1)}), bf16[4,8,3584]{2,1,0:T(8,128)(2,1)S(1)}, u32[]{:S(2)}, u32[]{:S(2)}) async-start(bf16[4,8,3584]{2,1,0:T(8,128)(2,1)} %bitcast.596), calls=%async_computation.3 | async-start | bytes 458752 | tf_op jit(solution)/shard_map/all_to_all | solution.py:59
Sparse Core Ops, SparseCore 0:
  9.7 147.2 all-gather.11
  242.7 72.7 reduce-scatter.3
  317.9 27.0 reduce-scatter.5
  347.3 16.0 reduce-scatter.7
where the time goes:
time: 396 us; the launch traced here: 395 us
  waiting for transfers between devices  249 us (63%)
  blocking collectives  74.9 us (19%)
  matrix products  26.7 us (7%)
  between operations  17.1 us (4%)
  local copies, waits for them, and re-layouts  16.1 us (4%)
  other arithmetic  6.47 us (2%)
  starting transfers between devices  4.97 us (1%)
    all_gather x1, waiting for transfers between devices, per_device(): lax.all_gather(hidden, TOK, axis=0, tiled=True)  128 us
    reduce_scatter x3, waiting for transfers between devices, sum_in_order(): blocks = lax.psum_scatter(blocks, axes[k], scatter_dimension=0, tiled=True)  121 us
    all_gather x5, blocking collectives, all_in_one(): both, at, found = (lax.all_gather(jnp.concatenate(lines), axis), 0, {})  57.3 us
    unnamed x1, blocking collectives  17.6 us
    unnamed x17, local copies, waits for them, and re-layouts  11.4 us
    dot_general x1, matrix products, per_device(): lax.dot_general(all_hidden, dlogits, (((0,), (0,)), ((), ())), preferred_...  9.57 us
    dot_general x1, matrix products, per_device(): jnp.dot(all_hidden, student_head, preferred_element_type=jnp.float32)  8.63 us
    dot_general x1, matrix products, per_device(): lax.dot_general(dlogits, student_head, (((1,), (1,)), ((), ())), preferre...  8.51 us
  transfers between devices with their start and end apart: 5, of which 4 were waited for; matrix products, arithmetic and copies ran while one was open for 5% of the time, Pallas kernels for 0%

commit v1 on v0

--- a/solution.py
+++ b/solution.py
@@ -7,6 +7,13 @@
 TOK = ("tok_0", "tok_1", "tok_2")
 TOK_VOC = ("tok_0", "tok_1", "tok_2", "voc_0", "voc_1")
 VOC = ("voc_0", "voc_1")
+
+
+def all_by_exchange(array, axis, dim):
+    size = lax.axis_size(axis)
+    blocks = jnp.stack([array for _ in range(size)])
+    blocks = lax.all_to_all(blocks, axis, split_axis=0, concat_axis=0)
+    return jnp.concatenate(blocks, axis=dim)
 
 
 def all_in_one(shard, axis):
@@ -83,7 +90,7 @@
 
 def per_device(hidden, teacher_logits, sampled_ids, loss_mask, student_head):
     all_hidden, all_ids, all_mask = (
-        lax.all_gather(hidden, TOK, axis=0, tiled=True),
+        all_by_exchange(hidden, TOK, 0),
         lax.all_gather(sampled_ids, TOK, axis=0, tiled=True),
         lax.all_gather(loss_mask, TOK, axis=0, tiled=True),
     )

time: 396 us -> 356 us (0.90)
  waiting for transfers between devices: 249 us -> 118 us
  blocking collectives: 74.9 us -> 151 us
  starting transfers between devices: 4.97 us -> 14.9 us
    all_gather x1 -> x0, waiting for transfers between devices: 128 us -> none  [per_device(): lax.all_gather(hidden, TOK, axis=0, tiled=True)]
    unnamed x1, blocking collectives: 17.6 us -> 108 us
    all_gather x5, blocking collectives: 57.3 us -> 43 us  [all_in_one(): both, at, found = (lax.all_gather(jnp.concatenate(lines), axis), 0, {})]
    all_to_all x0 -> x1, starting transfers between devices: none -> 9.96 us  [all_by_exchange(): blocks = lax.all_to_all(blocks, axis, split_axis=0, concat_axis=0)]
    another operation x0 -> x1, local copies, waits for them, and re-layouts: none -> 4.79 us  [all_by_exchange(): blocks = jnp.stack([array for _ in range(size)])]
  transfers between devices with their start and end apart: 5 -> 5, of which waited for: 4 -> 3; matrix products, arithmetic and copies ran while one was open for 5% -> 5% of each run, Pallas kernels for 0% -> 0%
where the time goes in v1:
time: 356 us; the launch traced here: 355 us
  blocking collectives  151 us (42%)
  waiting for transfers between devices  118 us (33%)
  matrix products  26.7 us (8%)
  local copies, waits for them, and re-layouts  19.9 us (6%)
  between operations  17.1 us (5%)
  starting transfers between devices  14.9 us (4%)
  other arithmetic  6.46 us (2%)
    reduce_scatter x3, waiting for transfers between devices, sum_in_order(): blocks = lax.psum_scatter(blocks, axes[k], scatter_dimension=0, tiled=True)  118 us
    unnamed x1, blocking collectives  108 us
    all_gather x5, blocking collectives, all_in_one(): both, at, found = (lax.all_gather(jnp.concatenate(lines), axis), 0, {})  43 us
    unnamed x17, local copies, waits for them, and re-layouts  10.5 us
    all_to_all x1, starting transfers between devices, all_by_exchange(): blocks = lax.all_to_all(blocks, axis, split_axis=0, concat_axis=0)  9.96 us
    dot_general x1, matrix products, per_device(): lax.dot_general(all_hidden, dlogits, (((0,), (0,)), ((), ())), preferred_...  9.54 us
    dot_general x1, matrix products, per_device(): jnp.dot(all_hidden, student_head, preferred_element_type=jnp.float32)  8.64 us
    dot_general x1, matrix products, per_device(): lax.dot_general(dlogits, student_head, (((1,), (1,)), ((), ())), preferre...  8.5 us
  transfers between devices with their start and end apart: 5, of which 3 were waited for; matrix products, arithmetic and copies ran while one was open for 5% of the time, Pallas kernels for 0%

profile of v1, /device:TPU:1, one launch (start us, length us, event | category | flops | bytes accessed | tf_op | source)
XLA Modules:
  0.0 355.0 jit_solution(16312167515455385034)
XLA Ops:
  7.2 4.8 %stack.2 = bf16[32,32,3584]{2,1,0:T(8,128)(2,1)} broadcast(bf16[32,3584]{1,0:T(8,128)(2,1)} %param.5), dimensions={1,2} | broadcast | bytes 7569408 | tf_op jit(solution)/shard_map/stack | solution.py:14
  12.0 0.0 copy-start.1
  12.0 10.0 %all-to-all-start = ((bf16[32,32,3584]{2,1,0:T(8,128)(2,1)}), bf16[32,32,3584]{2,1,0:T(8,128)(2,1)}, u32[]{:S(2)}, u32[]{:S(2)}) async-start(bf16[32,32,3584]{2,1,0:T(8,128)(2,1)} %stack.2), calls=%async_computation | async-start | bytes 14680064 | tf_op jit(solution)/shard_map/all_to_all | solution.py:15
  21.9 0.0 copy-start.4
  21.9 0.0 copy-start.2
  21.9 0.0 copy-start.3
  22.0 0.0 reduce-scatter.4.cloned.1.call-start
  22.0 0.0 copy-done.1
  22.0 0.7 copy.14
  22.7 0.2 reduce_max.28
  22.9 0.0 copy-done.4
  23.0 0.6 dynamic-slice
  24.2 0.0 copy-done.2
  24.2 0.2 dynamic-update-slice
  24.5 0.0 copy-done.3
  24.5 0.2 dynamic-update-slice.1
  24.7 108.4 %all-reduce.2 = (s32[1024]{0:T(1024)S(1)}, s32[1024]{0:T(1024)S(1)}) all-reduce(s32[1024]{0:T(1024)S(1)} %dynamic-update-slice, s32[1024]{0:T(1024)S(1)} %dynamic-update-slice.1), channel_id=1, replica_groups=mesh['tok_0'=2,'tok_1'=4,'tok_2'=4,'voc_0'=2,'voc_1'=2] {'tok_0','tok_1'..., use_global_device_ids=true, to_apply=%add | all-reduce | flops 2048 | bytes 16384
  133.2 0.0 all-to-all-done
  133.2 8.6 %fusion.119 = (f32[1024]{0:T(1024)S(1)}, f32[1024,640]{0,1:T(8,128)S(1)}) fusion(bf16[1024,3584]{1,0:T(8,128)(2,1)} %bitcast.1, bf16[3584,640]{1,0:T(8,128)(2,1)} %param.9), kind=kOutput, calls=%fused_computation.224 | convolution fusion | flops 4698274816 | bytes 14553088 | tf_op jit(solution)/shard_map/dot_general | solution.py:98
  141.8 0.0 copy-start
  141.8 1.5 copy-done
  143.3 1.8 fusion.3
  145.1 0.1 concatenate.15
  145.2 3.4 all-gather.5
  148.7 0.1 concatenate.16
  148.8 10.7 %all-gather.6 = f32[4,7,1024]{2,1,0:T(8,128)S(1)} all-gather(f32[1,7,1024]{2,1,0:T(8,128)S(1)} %bitcast.599), channel_id=3, replica_groups=mesh['tok_0'=2,'tok_1'=4,'tok_2'=4,'voc_0'=2,'voc_1'=2] {'tok_1'}, dimensions={0}, use_global_device_ids=true | all-gather | bytes 143360 | tf_op jit(solution)/shard_map/all_gather | solution.py:27
  159.5 0.1 fusion.55
  159.6 0.1 fusion.73
  159.7 0.1 concatenate.17
  159.7 9.2 %all-gather.7 = f32[4,7,1024]{2,1,0:T(8,128)S(1)} all-gather(f32[1,7,1024]{2,1,0:T(8,128)S(1)} %bitcast.600), channel_id=4, replica_groups=mesh['tok_0'=2,'tok_1'=4,'tok_2'=4,'voc_0'=2,'voc_1'=2] {'tok_2'}, dimensions={0}, use_global_device_ids=true | all-gather | bytes 143360 | tf_op jit(solution)/shard_map/all_gather | solution.py:27
  169.0 0.1 fusion.26
  169.1 0.1 fusion.44
  169.1 0.1 concatenate.18
  169.2 4.9 %all-gather.8 = f32[2,7,1024]{2,1,0:T(8,128)S(1)} all-gather(f32[1,7,1024]{2,1,0:T(8,128)S(1)} %bitcast.601), channel_id=5, replica_groups=mesh['tok_0'=2,'tok_1'=4,'tok_2'=4,'voc_0'=2,'voc_1'=2] {'voc_0'}, dimensions={0}, use_global_device_ids=true | all-gather | bytes 86016 | tf_op jit(solution)/shard_map/all_gather | solution.py:27
  174.2 0.1 concatenate.19
  174.3 14.8 %all-gather.9 = f32[2,7,1024]{2,1,0:T(8,128)S(1)} all-gather(f32[1,7,1024]{2,1,0:T(8,128)S(1)} %bitcast.602), channel_id=6, replica_groups=mesh['tok_0'=2,'tok_1'=4,'tok_2'=4,'voc_0'=2,'voc_1'=2] {'voc_1'}, dimensions={0}, use_global_device_ids=true | all-gather | bytes 86016 | tf_op jit(solution)/shard_map/all_gather | solution.py:27
  189.1 0.6 convert_reduce_fusion
  189.7 2.6 fusion.10
  192.3 8.5 %convolution_convert_fusion = bf16[1024,3584]{1,0:T(8,128)(2,1)S(1)} fusion(bf16[1024,640]{0,1:T(8,128)(2,1)S(1)} %fusion.10, bf16[3584,640]{1,0:T(8,128)(2,1)} %param.9), kind=kOutput, calls=%fused_computation | convolution fusion | flops 4701290496 | bytes 13238272 | tf_op jit(solution)/shard_map/dot_general | solution.py:142
  200.8 3.8 %copy.15 = bf16[2,4,4,32,3584]{4,3,0,2,1:T(8,128)(2,1)} copy(bf16[2,4,4,32,3584]{4,3,2,1,0:T(8,128)(2,1)S(1)} %bitcast.596) | data formatting | bytes 14680064 | tf_op jit(solution)/shard_map/reshape;reshape | solution.py:47
  204.6 0.0 reduce-scatter.4.cloned.1.call-update
  204.6 0.0 reduce-scatter.6.cloned.1.call-start
  204.7 70.4 %reduce-scatter.4.cloned.1.call-done = bf16[8,32,3584]{2,1,0:T(8,128)(2,1)} async-done(((bf16[32,32,3584]{2,1,0:T(8,128)(2,1)}), bf16[8,32,3584]{2,1,0:T(8,128)(2,1)}) %reduce-scatter.4.cloned.1.call-update) | async-done | bytes 1835024 | tf_op jit(solution)/shard_map/reduce_scatter | solution.py:50
  275.1 0.0 reduce-scatter.6.cloned.1.call-update
  275.1 0.0 reduce-scatter.8.cloned.1.call-start
  275.2 29.5 %reduce-scatter.6.cloned.1.call-done = bf16[2,32,3584]{2,1,0:T(8,128)(2,1)} async-done(((bf16[8,32,3584]{2,1,0:T(8,128)(2,1)}), bf16[2,32,3584]{2,1,0:T(8,128)(2,1)}) %reduce-scatter.6.cloned.1.call-update) | async-done | bytes 458768 | tf_op jit(solution)/shard_map/reduce_scatter | solution.py:50
  304.6 0.0 reduce-scatter.8.cloned.1.call-update
  304.7 18.5 %reduce-scatter.8.cloned.1.call-done = bf16[1,32,3584]{2,1,0:T(8,128)(2,1)} async-done(((bf16[2,32,3584]{2,1,0:T(8,128)(2,1)}), bf16[1,32,3584]{2,1,0:T(8,128)(2,1)}) %reduce-scatter.8.cloned.1.call-update) | async-done | bytes 229392 | tf_op jit(solution)/shard_map/reduce_scatter | solution.py:50
  323.1 4.8 %all-to-all-start.1 = ((bf16[4,8,3584]{2,1,0:T(8,128)(2,1)}), bf16[4,8,3584]{2,1,0:T(8,128)(2,1)S(1)}, u32[]{:S(2)}, u32[]{:S(2)}) async-start(bf16[4,8,3584]{2,1,0:T(8,128)(2,1)} %bitcast.597), calls=%async_computation.4 | async-start | bytes 458752 | tf_op jit(solution)/shard_map/all_to_all | solution.py:66
  328.0 9.5 %fusion = bf16[3584,640]{0,1:T(8,128)(2,1)} fusion(bf16[1024,640]{0,1:T(8,128)(2,1)S(1)} %fusion.10, bf16[1024,3584]{1,0:T(8,128)(2,1)} %bitcast.1), kind=kOutput, calls=%fused_computation.2 | convolution fusion | flops 4699914240 | bytes 13238272 | tf_op jit(solution)/shard_map/dot_general | solution.py:151
  337.5 7.2 %copy.16 = bf16[3584,640]{1,0:T(8,128)(2,1)} copy(bf16[3584,640]{0,1:T(8,128)(2,1)} %fusion) | data formatting | bytes 9175040
  346.1 0.6 dynamic_slice.3
  346.7 0.0 all-to-all-done.1
  346.7 0.7 reduce_sum.82
  (15 shorter events, 0.3 us)
Async XLA Ops:
  12.0 10.1 %copy-start.1 = (bf16[1024,640]{1,0:T(8,128)(2,1)S(1)}, bf16[1024,640]{1,0:T(8,128)(2,1)}, u32[]{:S(2)}) copy-start(bf16[1024,640]{1,0:T(8,128)(2,1)} %param.6) | copy-start | bytes 3932164
  12.0 121.2 %all-to-all-start = ((bf16[32,32,3584]{2,1,0:T(8,128)(2,1)}), bf16[32,32,3584]{2,1,0:T(8,128)(2,1)}, u32[]{:S(2)}, u32[]{:S(2)}) async-start(bf16[32,32,3584]{2,1,0:T(8,128)(2,1)} %stack.2), calls=%async_computation | async-start | bytes 14680064 | tf_op jit(solution)/shard_map/all_to_all | solution.py:15
  21.9 1.0 copy-start.4
  21.9 2.3 copy-start.2
  21.9 2.5 copy-start.3
  22.0 253.1 %reduce-scatter.4.cloned.1.call-start = ((), (), s32[]{:S(2)}) async-start(), calls=%async_computation.5 | async-start | bytes 9175040 | tf_op jit(solution)/shard_map/reduce_scatter | solution.py:50
  141.8 1.5 copy-start
  204.6 100.0 %reduce-scatter.6.cloned.1.call-start = ((), (), s32[]{:S(2)}) async-start(), calls=%async_computation.6 | async-start | bytes 2293760 | tf_op jit(solution)/shard_map/reduce_scatter | solution.py:50
  275.1 48.0 %reduce-scatter.8.cloned.1.call-start = ((), (), s32[]{:S(2)}) async-start(), calls=%async_computation.7 | async-start | bytes 688128 | tf_op jit(solution)/shard_map/reduce_scatter | solution.py:50
  323.1 23.5 %all-to-all-start.1 = ((bf16[4,8,3584]{2,1,0:T(8,128)(2,1)}), bf16[4,8,3584]{2,1,0:T(8,128)(2,1)S(1)}, u32[]{:S(2)}, u32[]{:S(2)}) async-start(bf16[4,8,3584]{2,1,0:T(8,128)(2,1)} %bitcast.597), calls=%async_computation.4 | async-start | bytes 458752 | tf_op jit(solution)/shard_map/all_to_all | solution.py:66
Sparse Core Ops, SparseCore 0:
  204.7 70.3 reduce-scatter.3
  277.5 27.0 reduce-scatter.5
  307.0 16.0 reduce-scatter.7
